TPU v7x, 32 devices: a whole 2x2x4 slice. The times are simulated.
32 devices in a mesh: seq: 16 (over z, y, x), mp: 2 (over core).
Axes of the slice: x: 2, y: 2, z: 4, core: 2. Of those that a mesh axis runs over, the one named last changes fastest.
Arguments:
- states: bfloat16 [4096, 768], P('seq'), may hold values from -24 to 24
- qkv_weight: bfloat16 [3, 768, 768], P(None, None, 'mp'), may hold values from -0.21875 to 0.21875
- out_weight: bfloat16 [768, 768], P('mp'), may hold values from -0.21875 to 0.21875
- up_weight: bfloat16 [768, 3072], P(None, 'mp'), may hold values from -0.21875 to 0.21875
- down_weight: bfloat16 [3072, 768], P('mp'), may hold values from -0.109375 to 0.109375
- attn_gain: float32 [768], replicated, may hold values from 0.5 to 1.5
- mlp_gain: float32 [768], replicated, may hold values from 0.5 to 1.5
- global_ids: int32 [2], replicated, may hold values from 0 to 63, as said below
- random_owner: int32 [2, 64, 6, 3], P('mp', 'seq'), may hold values from 0 to 15, all different within a row; in each aligned block of 24 rows (0 to 23, 24 to 47, ..., all dimensions but the last counted through in order) at most 5 rows name the same one
- random_local: int32 [2, 64, 6, 3], P('mp', 'seq'), may hold values from 0 to 3
Outputs:
- layer_out: bfloat16 [4096, 768], P('seq')
Inputs may be any that keep to these rules, and one draw needn't show every extreme that they name: `global_ids`: 2 different block numbers; the second is 63. The random key block is random_owner * 4 + random_local. For one query block and head the 3 owners differ. Within the rows of one device (aligned blocks of 4 * K rows over the first three dimensions, K the third dimension) no owner is named more than 5 times, a bound that some block reaches.
All inputs are finite; a program needn't handle non-finite values.
Results may differ from a plain program's by a relative error of at most 0.008.
The roundings to bfloat16 on the way count: a program that leaves them out, or rounds other values in their place, can miss the bound.
Values may be sent and summed in bfloat16 or wider, within the bound.
A program may use at most 192 MiB of HBM per device.

v0:
```python
import jax
import jax.numpy as jnp
from jax import lax
from jax.sharding import PartitionSpec as P

HD = 64
BS = 64
R = 3


EPSILON = 1e-05
NEGATIVE = -1e30


def with_halo(cells, sides, width):
    for axis, dim in sides:
        count = lax.axis_size(axis)
        ends = count - 1
        head = lax.slice_in_dim(cells, 0, width, axis=dim)
        tail = lax.slice_in_dim(cells, cells.shape[dim] - width, cells.shape[dim], axis=dim)
        cells = jnp.concatenate(
            [
                lax.ppermute(tail, axis, [(i, (i + 1) % count) for i in range(ends)]),
                cells,
                lax.ppermute(head, axis, [((i + 1) % count, i) for i in range(ends)]),
            ],
            axis=dim,
        )
    return cells


def merged(value, axis, join):
    pieces = jax.tree.map(lambda part: lax.all_gather(part, axis), value)
    head = jax.tree.map(lambda part: part[0], pieces)
    tail = jax.tree.map(lambda part: part[1:], pieces)
    so_far, _ = lax.scan(lambda so_far, share: (join(so_far, share), None), head, tail)
    return so_far


def layer_norm(inputs, scales):
    center = jnp.mean(inputs, axis=-1, keepdims=True)
    shifted = inputs - center
    spread = jnp.mean(shifted * shifted, axis=-1, keepdims=True)
    return shifted * lax.rsqrt(spread + EPSILON) * scales


def merge_partials(earlier, later):
    high_early, total_early, acc_early = earlier
    high_late, total_late, acc_late = later
    highest = jnp.maximum(high_early, high_late)
    factor_early = jnp.exp(high_early - highest)
    factor_late = jnp.exp(high_late - highest)
    total = total_early * factor_early + total_late * factor_late
    summed = acc_early * factor_early[..., None] + acc_late * factor_late[..., None]
    return (highest, total, summed)


def shards(
    states,
    qkv_weight,
    out_weight,
    up_weight,
    down_weight,
    attn_gain,
    mlp_gain,
    global_ids,
    random_owner,
    random_local,
):
    tokens_here = states.shape[0]
    head_width = qkv_weight.shape[2]
    head_count = head_width // HD
    block_count = tokens_here // BS
    seq_count = lax.axis_size("seq")
    position = lax.axis_index("seq")
    first_block = position * block_count
    scaling = HD ** (-0.5)
    highest = lax.Precision.HIGHEST
    queries = jnp.dot(states, qkv_weight[0], preferred_element_type=jnp.float32).astype(
        jnp.bfloat16
    )
    query_blocks = queries.reshape(block_count, BS, head_count, HD)
    key_part = jnp.dot(states, qkv_weight[1], preferred_element_type=jnp.float32).astype(
        jnp.bfloat16
    )
    value_part = jnp.dot(states, qkv_weight[2], preferred_element_type=jnp.float32).astype(
        jnp.bfloat16
    )
    key_value = jnp.concatenate(
        [
            key_part.reshape(tokens_here, head_count, HD),
            value_part.reshape(tokens_here, head_count, HD),
        ],
        axis=2,
    )
    pair_blocks = key_value.reshape(block_count, BS, head_count, 2 * HD)
    owner_of = global_ids // block_count
    local_of = global_ids % block_count
    owned_mask = (owner_of == position).astype(jnp.float32)[:, None, None, None]
    local_query = query_blocks[local_of].astype(jnp.float32) * owned_mask
    local_pair = pair_blocks[local_of].astype(jnp.float32) * owned_mask
    summed_query, summed_pair = lax.psum((local_query, local_pair), "seq")
    global_query = summed_query.astype(jnp.bfloat16)
    global_pair = summed_pair.astype(jnp.bfloat16)
    padded = with_halo(key_value, (("seq", 0),), BS)
    padded = padded.reshape(block_count + 2, BS, head_count, 2 * HD)
    window = jnp.stack([padded[shift_by : shift_by + block_count] for shift_by in range(3)], axis=1)
    neighbour = (
        first_block
        + jnp.arange(block_count, dtype=jnp.int32)[:, None]
        + jnp.arange(-1, 2, dtype=jnp.int32)[None, :]
    )
    inside = (neighbour >= 0) & (neighbour < seq_count * block_count)
    score_window = (
        jnp.einsum(
            "bqhd,bwkhd->bhqwk", query_blocks, window[..., :HD], preferred_element_type=jnp.float32
        )
        * scaling
    )
    score_window = jnp.where(inside[:, None, None, :, None], score_window, NEGATIVE)
    score_global = (
        jnp.einsum(
            "bqhd,gkhd->bhqgk",
            query_blocks,
            global_pair[..., :HD],
            preferred_element_type=jnp.float32,
        )
        * scaling
    )
    owner_list = random_owner.reshape(-1)
    local_list = random_local.reshape(-1)
    item_count = owner_list.shape[0]
    capacity = max(2, item_count // seq_count + 1)
    slot_total = seq_count * capacity
    head_list = jnp.broadcast_to(
        jnp.arange(head_count, dtype=jnp.int32)[None, :, None], (block_count, head_count, R)
    ).reshape(-1)
    matches = (owner_list[:, None] == jnp.arange(seq_count, dtype=jnp.int32)[None, :]).astype(
        jnp.int32
    )
    slot_rank = jnp.sum((jnp.cumsum(matches, axis=0) - matches) * matches, axis=1)
    slot_index = owner_list * capacity + slot_rank
    block_table = pair_blocks.transpose(0, 2, 1, 3).reshape(block_count * head_count, BS, 2 * HD)
    wanted = (
        jnp.zeros((slot_total,), jnp.int32).at[slot_index].set(local_list * head_count + head_list)
    )
    wanted = wanted.reshape(seq_count, capacity)
    remote = lax.all_to_all(
        block_table[lax.all_to_all(wanted, "seq", split_axis=0, concat_axis=0, tiled=True)],
        "seq",
        split_axis=0,
        concat_axis=0,
        tiled=True,
    ).reshape(slot_total, BS, 2 * HD)[slot_index]
    remote = remote.reshape(block_count, head_count, R, BS, 2 * HD)
    score_random = (
        jnp.einsum(
            "bqhd,bhrkd->bhqrk", query_blocks, remote[..., :HD], preferred_element_type=jnp.float32
        )
        * scaling
    )
    joined = jnp.concatenate([score_window, score_random, score_global], axis=3)
    joined_shape = joined.shape
    flat_scores = joined.reshape(joined_shape[0], joined_shape[1], joined_shape[2], -1)
    row_high = jnp.max(flat_scores, axis=-1, keepdims=True)
    raised = jnp.exp(flat_scores - row_high)
    weights = (
        (raised / jnp.sum(raised, axis=-1, keepdims=True))
        .astype(jnp.bfloat16)
        .reshape(joined_shape)
    )
    mixed = jnp.einsum(
        "bhqwk,bwkhd->bqhd",
        weights[:, :, :, :3],
        window[..., HD:],
        preferred_element_type=jnp.float32,
    )
    mixed = mixed + jnp.einsum(
        "bhqrk,bhrkd->bqhd",
        weights[:, :, :, 3 : 3 + R],
        remote[..., HD:],
        preferred_element_type=jnp.float32,
    )
    mixed = mixed + jnp.einsum(
        "bhqgk,gkhd->bqhd",
        weights[:, :, :, 3 + R :],
        global_pair[..., HD:],
        preferred_element_type=jnp.float32,
    )
    global_scores = (
        jnp.einsum(
            "gqhd,khd->hgqk",
            global_query,
            key_part.reshape(tokens_here, head_count, HD),
            preferred_element_type=jnp.float32,
        )
        * scaling
    )
    local_high = jnp.max(global_scores, axis=-1)
    global_raised = jnp.exp(global_scores - local_high[..., None])
    local_total = jnp.sum(global_raised, axis=-1)
    local_acc = jnp.einsum(
        "hgqk,khd->hgqd",
        global_raised,
        value_part.reshape(tokens_here, head_count, HD).astype(jnp.float32),
        precision=highest,
    )
    merged_high, merged_total, merged_acc = merged(
        (local_high, local_total, local_acc), "seq", merge_partials
    )
    global_out = merged_acc / merged_total[..., None]
    placed_here = (
        global_ids[:, None] == first_block + jnp.arange(block_count, dtype=jnp.int32)[None, :]
    ).astype(jnp.float32)
    keep_rows = 1.0 - jnp.sum(placed_here, axis=0)
    placed = jnp.einsum("gb,hgqd->bqhd", placed_here, global_out, precision=highest)
    attended = (
        (mixed * keep_rows[:, None, None, None] + placed)
        .astype(jnp.bfloat16)
        .reshape(tokens_here, head_width)
    )
    projected = lax.psum(jnp.dot(attended, out_weight, preferred_element_type=jnp.float32), "mp")
    normed = layer_norm(states.astype(jnp.float32) + projected, attn_gain).astype(jnp.bfloat16)
    hidden = jax.nn.gelu(
        jnp.dot(normed, up_weight, preferred_element_type=jnp.float32), approximate=False
    ).astype(jnp.bfloat16)
    expanded = lax.psum(jnp.dot(hidden, down_weight, preferred_element_type=jnp.float32), "mp")
    return layer_norm(normed.astype(jnp.float32) + expanded, mlp_gain).astype(jnp.bfloat16)


def solution(mesh):
    in_specs = (
        P("seq", None),
        P(None, None, "mp"),
        P("mp", None),
        P(None, "mp"),
        P("mp", None),
        P(),
        P(),
        P(),
        P("mp", "seq", None, None),
        P("mp", "seq", None, None),
    )
    out_specs = P("seq", None)
    return jax.shard_map(shards, mesh=mesh, in_specs=in_specs, out_specs=out_specs, check_vma=False)
```

profile of v0, /device:TPU:31, one launch (start us, length us, event | category | flops | bytes accessed | tf_op | source)
XLA Modules:
  0.0 393.5 jit_solution(6422734650747979945)
XLA Ops:
  22.1 68.3 %all-reduce.8 = (bf16[2,64,6,128]{3,1,0,2:T(8,128)(2,1)}, bf16[2,64,6,64]{3,1,0,2:T(8,128)(2,1)}) all-reduce(f32[2,64,6,128]{3,1,0,2:T(8,128)S(1)} %convert_multiply_fusion.1, f32[2,64,6,64]{3,1,0,2:T(8,128)S(1)} %convert_multiply_fusion), channel_id=1, replica_groups=mesh['seq'=16,'mp'=2] {'seq'}, use_global_device_ids=true, to_apply=%region_3.4 | all-reduce | flops 147456 | bytes 884736 | tf_op jit(solution)/shard_map/psum | solution.py:102
  91.7 2.3 fusion.29
  110.5 9.2 %all_to_all.17 = s32[16,1,5]{2,1,0:T(1,128)} all-to-all(s32[16,1,5]{2,1,0:T(1,128)S(1)} %bitcast.147), channel_id=1, replica_groups=mesh['seq'=16,'mp'=2] {'seq'}, dimensions={0} | all-to-all | bytes 640 | tf_op jit(solution)/shard_map/all_to_all | solution.py:149
  123.1 1.9 gather_fusion
  125.0 9.2 %all-to-all-start.1 = ((bf16[16,5,64,128]{3,2,1,0:T(8,128)(2,1)}), bf16[16,5,64,128]{3,2,1,0:T(8,128)(2,1)}, u32[]{:S(2)}, u32[]{:S(2)}) async-start(bf16[16,5,64,128]{3,2,1,0:T(8,128)(2,1)} %bitcast.135), calls=%async_computation.1 | async-start | bytes 2621440 | tf_op jit(solution)/shard_map/all_to_all | solution.py:148
  136.5 4.7 %collective-permute-start.1 = (bf16[64,6,128]{0,2,1:T(8,128)(2,1)}, bf16[64,6,128]{0,2,1:T(8,128)(2,1)}, u32[]{:S(2)}, u32[]{:S(2)}) collective-permute-start(bf16[64,6,128]{0,2,1:T(8,128)(2,1)} %get-tuple-element.70), channel_id=1, source_target_pairs={{2,0},{4,2},{6,4},{8,6},{10,8},{12,10},{14,12},{16,14},{18,16},{20... | collective-permute-start | bytes 294920 | tf_op jit(solution)/shard_map/ppermute | solution.py:25
  141.2 2.0 reshape.265
  143.2 2.0 reshape.264
  145.2 56.8 %all-gather = f32[96,2,64]{2,1,0:T(2,128)S(1)} all-gather(f32[6,2,64]{2,1,0:T(2,128)S(1)} %get-tuple-element.75), channel_id=2, replica_groups=mesh['seq'=16,'mp'=2] {'seq'}, dimensions={0}, use_global_device_ids=true | all-gather | bytes 52224 | tf_op jit(solution)/shard_map/all_gather | solution.py:33
  203.0 30.2 %all-gather.1 = f32[96,2,64]{2,1,0:T(2,128)S(1)} all-gather(f32[6,2,64]{2,1,0:T(2,128)S(1)} %fusion.30), channel_id=3, replica_groups=mesh['seq'=16,'mp'=2] {'seq'}, dimensions={0}, use_global_device_ids=true | all-gather | bytes 52224 | tf_op jit(solution)/shard_map/all_gather | solution.py:33
  234.2 2.0 copy.76
  236.3 1.9 copy.75
  239.5 2.3 fusion.84
  246.8 2.4 fusion.83
  249.2 2.2 gather_fusion.1
  258.6 2.0 fusion.19
  260.6 6.2 %slice.124 = f32[90,2,64,64]{3,2,1,0:T(8,128)} slice(f32[96,2,64,64]{3,2,1,0:T(8,128)} %all-gather.5.cloned.1.call-done), slice={[6:96], [0:2], [0:64], [0:64]} | slice | bytes 5898240 | tf_op jit(solution)/shard_map/slice | solution.py:35
  266.9 31.8 %while.14 = (s32[]{:T(128)}, f32[6,2,64]{2,1,0:T(2,128)S(1)}, f32[6,2,64]{2,1,0:T(2,128)S(1)}, f32[6,2,64,64]{3,2,1,0:T(8,128)S(1)}, f32[15,6,2,64]{3,2,1,0:T(2,...) while((s32[]{:T(128)}, f32[6,2,64]{2,1,0:T(2,128)S(1)}, ...), condition=%wide.region_13.14_spmd, body=%wide.region_12.13_spmd.sunk | while | flops 152066 | bytes 620645 | solution.py:36
  298.9 2.0 fusion.37
  302.3 1.8 fusion.20
  304.8 2.4 fusion.90
  307.4 47.7 %all-reduce.5.cloned.1.call-done = f32[256,768]{1,0:T(8,128)} async-done(((f32[256,768]{1,0:T(8,128)}), f32[256,768]{1,0:T(8,128)}) %all-reduce.5.cloned.1.call-update) | async-done | bytes 786448 | tf_op jit(solution)/shard_map/psum | solution.py:222
  356.9 7.2 %fusion.27 = f32[256,768]{1,0:T(8,128)} fusion(bf16[1536,768]{1,0:T(8,128)(2,1)S(1)} %copy-done, bf16[256,768]{1,0:T(8,128)(2,1)S(1)} %multiply_convert_fusion.1, bf16[768,1536]{1,0:T(8,128)(2,1)} %param.15), kind=kOutput, calls=%fused_computation.66 | convolution fusion | flops 1233518592 | bytes 5898240 | tf_op jit(solution)/shard_map/dot_general | solution.py:227
  364.1 20.3 %all-reduce.7.cloned.1.call-done = f32[256,768]{1,0:T(8,128)} async-done(((f32[256,768]{1,0:T(8,128)}), f32[256,768]{1,0:T(8,128)}) %all-reduce.7.cloned.1.call-update) | async-done | bytes 786448 | tf_op jit(solution)/shard_map/psum | solution.py:227
  (200 shorter events, 92.5 us)
Async XLA Ops:
  6.5 350.4 %copy-start = (bf16[1536,768]{1,0:T(8,128)(2,1)S(1)}, bf16[1536,768]{1,0:T(8,128)(2,1)}, u32[]{:S(2)}) copy-start(bf16[1536,768]{1,0:T(8,128)(2,1)} %param.16) | copy-start | bytes 7077892
  6.5 254.1 %all-gather.5.cloned.1.call-start = ((), (), s32[]{:S(2)}) async-start(), calls=%async_computation.4 | async-start | bytes 6684672 | tf_op jit(solution)/shard_map/all_gather | solution.py:33
  8.2 5.9 %copy-start.20 = (bf16[256,384]{1,0:T(8,128)(2,1)}, bf16[256,384]{1,0:T(8,128)(2,1)S(1)}, u32[]{:S(2)}) copy-start(bf16[256,384]{1,0:T(8,128)(2,1)S(1)} %convolution_convert_fusion.2) | copy-start | bytes 589828
  125.0 9.2 %copy-start.13 = (bf16[256,384]{0,1:T(8,128)(2,1)S(1)}, bf16[256,384]{0,1:T(8,128)(2,1)}, u32[]{:S(2)}) copy-start(bf16[256,384]{0,1:T(8,128)(2,1)} %copy.70) | copy-start | bytes 589828
  125.0 9.2 %copy-start.15 = (bf16[256,384]{0,1:T(8,128)(2,1)S(1)}, bf16[256,384]{0,1:T(8,128)(2,1)}, u32[]{:S(2)}) copy-start(bf16[256,384]{0,1:T(8,128)(2,1)} %copy.71) | copy-start | bytes 589828
  125.0 124.3 %all-to-all-start.1 = ((bf16[16,5,64,128]{3,2,1,0:T(8,128)(2,1)}), bf16[16,5,64,128]{3,2,1,0:T(8,128)(2,1)}, u32[]{:S(2)}, u32[]{:S(2)}) async-start(bf16[16,5,64,128]{3,2,1,0:T(8,128)(2,1)} %bitcast.135), calls=%async_computation.1 | async-start | bytes 2621440 | tf_op jit(solution)/shard_map/all_to_all | solution.py:148
  134.1 220.9 %all-reduce.5.cloned.1.call-start = ((), (), s32[]{:S(2)}) async-start(), calls=%async_computation.2 | async-start | bytes 1572864 | tf_op jit(solution)/shard_map/psum | solution.py:222
  135.1 98.8 %copy-start.9 = (bf16[4,64,6,64]{1,0,3,2:T(4,128)(2,1)S(1)}, bf16[4,64,6,64]{1,0,3,2:T(4,128)(2,1)}, u32[]{:S(2)}) copy-start(bf16[4,64,6,64]{1,0,3,2:T(4,128)(2,1)} %copy-done.8) | copy-start | bytes 589828
  135.1 107.3 %collective-permute-start = (bf16[64,6,128]{0,2,1:T(8,128)(2,1)}, bf16[64,6,128]{0,2,1:T(8,128)(2,1)}, u32[]{:S(2)}, u32[]{:S(2)}) collective-permute-start(bf16[64,6,128]{0,2,1:T(8,128)(2,1)} %get-tuple-element.69), channel_id=1, source_target_pairs={{0,2},{2,4},{4,6},{6,8},{8,10},{10,12},{12,14},{14,16},{16,18},{18... | collective-permute-start | bytes 294920 | tf_op jit(solution)/shard_map/ppermute | solution.py:23
  136.5 105.9 %collective-permute-start.1 = (bf16[64,6,128]{0,2,1:T(8,128)(2,1)}, bf16[64,6,128]{0,2,1:T(8,128)(2,1)}, u32[]{:S(2)}, u32[]{:S(2)}) collective-permute-start(bf16[64,6,128]{0,2,1:T(8,128)(2,1)} %get-tuple-element.70), channel_id=1, source_target_pairs={{2,0},{4,2},{6,4},{8,6},{10,8},{12,10},{14,12},{16,14},{18,16},{20... | collective-permute-start | bytes 294920 | tf_op jit(solution)/shard_map/ppermute | solution.py:25
  203.0 35.2 %copy-start.30 = (s32[2]{0:T(128)S(1)}, s32[2]{0:T(128)}, u32[]{:S(2)}) copy-start(s32[2]{0:T(128)} %param.19) | copy-start | bytes 28
  203.0 36.4 %copy-start.22 = (bf16[2,64,6,128]{3,1,0,2:T(8,128)(2,1)S(1)}, bf16[2,64,6,128]{3,1,0,2:T(8,128)(2,1)}, u32[]{:S(2)}) copy-start(bf16[2,64,6,128]{3,1,0,2:T(8,128)(2,1)} %get-tuple-element.59) | copy-start | bytes 589828
  234.2 7.6 %copy-start.12 = (bf16[4,64,6,64,1]{3,1,4,2,0:T(8,128)(2,1)}, bf16[4,64,6,64,1]{3,1,4,2,0:T(8,128)(2,1)S(1)}, u32[]{:S(2)}) copy-start(bf16[4,64,6,64,1]{3,1,4,2,0:T(8,128)(2,1)S(1)} %copy.107) | copy-start | bytes 589828
  236.3 5.5 %copy-start.37 = (s32[72]{0:T(128)S(1)}, s32[72]{0:T(128)}, u32[]{:S(2)}) copy-start(s32[72]{0:T(128)} %copy-done.36) | copy-start | bytes 868
  236.3 6.1 %copy-start.14 = (bf16[256,384]{0,1:T(8,128)(2,1)S(1)}, bf16[256,384]{0,1:T(8,128)(2,1)}, u32[]{:S(2)}) copy-start(bf16[256,384]{0,1:T(8,128)(2,1)} %copy.70) | copy-start | bytes 589828
  236.3 6.1 %copy-start.16 = (bf16[256,384]{0,1:T(8,128)(2,1)S(1)}, bf16[256,384]{0,1:T(8,128)(2,1)}, u32[]{:S(2)}) copy-start(bf16[256,384]{0,1:T(8,128)(2,1)} %copy.71) | copy-start | bytes 589828
  260.6 6.2 %slice-start = ((f32[96,2,64,64]{3,2,1,0:T(8,128)}), f32[6,2,64,64]{3,2,1,0:T(8,128)S(1)}, s32[]{:S(2)}) async-start(f32[96,2,64,64]{3,2,1,0:T(8,128)} %all-gather.5.cloned.1.call-done), calls=%async_computation.5 | async-start | bytes 786432 | tf_op jit(solution)/shard_map/slice | solution.py:34
  260.6 6.2 %slice-start.1 = ((f32[96,2,64]{2,1,0:T(2,128)}), f32[90,2,64]{2,1,0:T(2,128)S(1)}, s32[]{:S(2)}) async-start(f32[96,2,64]{2,1,0:T(2,128)} %copy-done.24), calls=%async_computation.6 | async-start | bytes 184320 | tf_op jit(solution)/shard_map/slice | solution.py:35
  266.9 32.0 %copy-start.31 = (s32[2]{0:T(128)S(1)}, s32[2]{0:T(128)}, u32[]{:S(2)}) copy-start(s32[2]{0:T(128)} %param.19) | copy-start | bytes 28
  266.9 32.0 %copy-start.34 = (s32[4]{0:T(128)S(1)}, s32[4]{0:T(128)}, u32[]{:S(2)}) copy-start(s32[4]{0:T(128)} %copy-done.33) | copy-start | bytes 52
  304.5 50.6 %copy-start.11 = (bf16[256,768]{1,0:T(8,128)(2,1)S(1)}, bf16[256,768]{1,0:T(8,128)(2,1)}, u32[]{:S(2)}) copy-start(bf16[256,768]{1,0:T(8,128)(2,1)} %param.12) | copy-start | bytes 1179652
  307.1 49.6 %copy-start.27 = (f32[768]{0:T(1024)S(1)}, f32[768]{0:T(1024)}, u32[]{:S(2)}) copy-start(f32[768]{0:T(1024)} %param.17) | copy-start | bytes 9220
  307.2 77.3 %all-reduce.7.cloned.1.call-start = ((), (), s32[]{:S(2)}) async-start(), calls=%async_computation.3 | async-start | bytes 1572864 | tf_op jit(solution)/shard_map/psum | solution.py:227
  364.1 22.0 %copy-start.28 = (f32[768]{0:T(1024)S(1)}, f32[768]{0:T(1024)}, u32[]{:S(2)}) copy-start(f32[768]{0:T(1024)} %param.18) | copy-start | bytes 9220
  (22 other events, 56.3 us)
Sparse Core Ops, SparseCore 0:
  94.1 125.6 all-gather.4
  307.3 47.7 all-reduce.4
  364.2 20.1 all-reduce.6
where the time goes:
time: 397 us; the launch traced here: 394 us
  blocking collectives  164 us (41%)
  waiting for transfers between devices  68 us (17%)
  other arithmetic  57.4 us (14%)
  local copies, waits for them, and re-layouts  44.7 us (11%)
  matrix products  29.3 us (7%)
  starting transfers between devices  15.6 us (4%)
  between operations  13.7 us (3%)
    all_gather x2, blocking collectives, merged(): pieces = jax.tree.map(lambda part: lax.all_gather(part, axis), value)  87 us
    psum x1, blocking collectives, shards(): summed_query, summed_pair = lax.psum((local_query, local_pair), 'seq')  68.3 us
    psum x1, waiting for transfers between devices, shards(): lax.psum(jnp.dot(attended, out_weight, preferred_element_type=jnp.float32...  47.7 us
    add x15, other arithmetic, merge_partials(): acc_early * factor_early[..., None] + acc_late * factor_late[..., None]  20.6 us
    psum x1, waiting for transfers between devices, shards(): lax.psum(jnp.dot(hidden, down_weight, preferred_element_type=jnp.float32)...  20.3 us
    concatenate x8, local copies, waits for them, and re-layouts, shards(): jnp.concatenate([key_part.reshape(tokens_here, head_count, HD), value_par...  11.4 us
    add x15, other arithmetic, merge_partials(): total = total_early * factor_early + total_late * factor_late  10.8 us
    all_to_all x1, blocking collectives, shards(): lax.all_to_all(wanted, 'seq', split_axis=0, concat_axis=0, tiled=True)  9.2 us
  transfers between devices with their start and end apart: 6, of which 2 were waited for; matrix products, arithmetic and copies ran while one was open for 13% of the time, Pallas kernels for 0%

commit v1 on v0

v1 whole, which is shorter than its diff:
```python
import functools

import jax
import jax.numpy as jnp
from jax import lax
from jax.experimental import pallas as pl
from jax.experimental.pallas import tpu as pltpu
from jax.sharding import PartitionSpec as P

HD = 64
BS = 64
R = 3
LANES = 128
MESH = pl.DeviceIdType.MESH

EPSILON = 1e-05
NEGATIVE = -1e30


def layer_norm(inputs, scales):
    center = jnp.mean(inputs, axis=-1, keepdims=True)
    shifted = inputs - center
    spread = jnp.mean(shifted * shifted, axis=-1, keepdims=True)
    return shifted * lax.rsqrt(spread + EPSILON) * scales


def dot_t(a, b):
    return lax.dot_general(a, b, (((1,), (1,)), ((), ())), preferred_element_type=jnp.float32)


def dot(a, b):
    return jnp.dot(a, b, preferred_element_type=jnp.float32)


def swap_halves(x):
    return pltpu.roll(x, HD, 1)


def attend_kernel(
    n,
    cap,
    heads,
    blocks,
    g_count,
    states,
    weight,
    wanted,
    slot,
    gids,
    att,
    tab,
    tab_s,
    cand,
    cand_in,
    pick,
    gath,
    gstates,
    kvb,
    qpad,
    stage,
    rr,
    halo_l,
    halo_r,
    win,
    gq,
    gkv,
    part,
    part_in,
    gmine,
    gout,
    s_tab,
    r_tab,
    s_cand,
    r_cand,
    s_gath,
    r_gath,
    s_rand,
    r_rand,
    s_halo,
    r_halo,
    s_part,
    r_part,
    s_gout,
    r_gout,
    l_sem,
):
    me = lax.axis_index("seq")
    pairs = heads // 2
    width = states.shape[1]
    cols = width // LANES
    quarters = BS // 16
    units = g_count * cols * quarters
    per = cand_in.shape[1]
    cand_parts = units // per
    rows_per = part_in.shape[1]
    part_parts = part.shape[0] // rows_per
    left = lax.rem(me + n - 1, n)
    right = lax.rem(me + 1, n)

    def peer(k):
        return lax.rem(me + k, n)

    def each_peer(body):
        def step(k, carry):
            body(peer(k))
            return carry

        lax.fori_loop(1, n, step, 0)

    def guarded(limit, who, body):
        if limit < n:
            pl.when(who < limit)(body)
        else:
            body()

    def remote(src, dst, ssem, rsem, d):
        return pltpu.make_async_remote_copy(
            src_ref=src,
            dst_ref=dst,
            send_sem=ssem,
            recv_sem=rsem,
            device_id={"seq": d},
            device_id_type=MESH,
        )

    def tab_copy(d, owner):
        return remote(wanted.at[d], tab.at[owner], s_tab.at[d], r_tab.at[owner], d)

    def cand_copy(d, owner):
        return remote(
            cand.at[pl.ds(d * per, per)], cand_in.at[owner], s_cand.at[d], r_cand.at[owner], d
        )

    def gath_copy(d, owner):
        return remote(
            pick, gath.at[pl.ds(owner * per, per)], s_gath.at[d], r_gath.at[owner], d
        )

    def rand_copy(d, owner):
        return remote(
            stage.at[pl.ds(d * cap, cap)],
            rr.at[pl.ds(owner * cap, cap)],
            s_rand.at[d],
            r_rand.at[owner],
            d,
        )

    def part_copy(d, owner):
        return remote(
            part.at[pl.ds(pl.multiple_of(d * rows_per, 8), rows_per)],
            part_in.at[owner],
            s_part.at[d],
            r_part.at[owner],
            d,
        )

    def gout_copy(d, owner):
        return remote(
            gmine,
            gout.at[pl.ds(pl.multiple_of(owner * rows_per, 8), rows_per)],
            s_gout.at[d],
            r_gout.at[owner],
            d,
        )

    to_right = remote(
        kvb.at[pl.ds((blocks - 1) * heads, heads)], halo_l, s_halo.at[0], r_halo.at[0], right
    )
    to_left = remote(kvb.at[pl.ds(0, heads)], halo_r, s_halo.at[1], r_halo.at[1], left)

    for g in range(g_count):
        local = lax.rem(gids[g], blocks)
        for j in range(cols):
            cut = slice(j * LANES, (j + 1) * LANES)
            piece = states[0:BS, cut]
            for b in range(1, blocks):
                piece = jnp.where(local == b, states[b * BS : (b + 1) * BS, cut], piece)
            for q in range(quarters):
                cand[(g * cols + j) * quarters + q] = piece[q * 16 : (q + 1) * 16]

    barrier = pltpu.get_barrier_semaphore()
    each_peer(
        lambda d: pl.semaphore_signal(barrier, inc=1, device_id={"seq": d}, device_id_type=MESH)
    )
    pl.semaphore_wait(barrier, n - 1)

    each_peer(lambda d: tab_copy(d, me).start())
    each_peer(lambda d: guarded(cand_parts, d, lambda: cand_copy(d, me).start()))
    tab[me] = wanted[me]

    def own_cand():
        cand_in[me] = cand[pl.ds(me * per, per)]

    guarded(cand_parts, me, own_cand)

    lane = lax.broadcasted_iota(jnp.int32, (BS, LANES), 1)
    low = lane < HD
    x = states[...]
    for j in range(pairs):
        cut = slice(j * LANES, (j + 1) * LANES)
        k = dot(x, weight[1, :, cut])
        v = dot(x, weight[2, :, cut])
        for b in range(blocks):
            kb, vb = k[b * BS : (b + 1) * BS], v[b * BS : (b + 1) * BS]
            kvb[b * heads + 2 * j] = jnp.where(low, kb, swap_halves(vb)).astype(jnp.bfloat16)
            kvb[b * heads + 2 * j + 1] = jnp.where(low, swap_halves(kb), vb).astype(jnp.bfloat16)

    to_right.start()
    to_left.start()

    each_peer(lambda d: tab_copy(d, d).wait_recv())
    table = pltpu.make_async_copy(tab, tab_s, l_sem)
    table.start()
    table.wait()

    def serve(d):
        for c in range(cap):
            stage[d * cap + c] = kvb[tab_s[d, 0, c]]
        rand_copy(d, me).start()

    each_peer(serve)
    for c in range(cap):
        rr[me * cap + c] = kvb[tab_s[me, 0, c]]

    def relay():
        each_peer(lambda d: cand_copy(d, d).wait_recv())
        for u in range(per):
            g = (me * per + u) // (cols * quarters)
            wanted_id = gids[g]

            def choose(d, so_far):
                here = (wanted_id >= d * blocks) & (wanted_id < (d + 1) * blocks)
                return jnp.where(here, cand_in[d, u], so_far)

            pick[u] = lax.fori_loop(1, n, choose, cand_in[0, u])
        gath[pl.ds(me * per, per)] = pick[...]
        each_peer(lambda d: gath_copy(d, me).start())

    guarded(cand_parts, me, relay)

    scaling = HD ** (-0.5)
    for j in range(pairs):
        cut = slice(j * LANES, (j + 1) * LANES)
        q = dot(x, weight[0, :, cut]).astype(jnp.bfloat16).astype(jnp.float32) * scaling
        for b in range(blocks):
            qb = q[b * BS : (b + 1) * BS]
            qpad[b * heads + 2 * j] = jnp.where(low, qb, 0.0).astype(jnp.bfloat16)
            qpad[b * heads + 2 * j + 1] = jnp.where(low, swap_halves(qb), 0.0).astype(jnp.bfloat16)

    each_peer(lambda d: guarded(cand_parts, d, lambda: gath_copy(d, d).wait_recv()))
    for g in range(g_count):
        for j in range(cols):
            for q in range(quarters):
                gstates[g * BS + q * 16 : g * BS + (q + 1) * 16, j * LANES : (j + 1) * LANES] = (
                    gath[(g * cols + j) * quarters + q]
                )
    gx = gstates[...]
    rows = g_count * BS
    glane = lax.broadcasted_iota(jnp.int32, (rows, LANES), 1)
    glow = glane < HD
    for j in range(pairs):
        cut = slice(j * LANES, (j + 1) * LANES)
        q = dot(gx, weight[0, :, cut]).astype(jnp.bfloat16).astype(jnp.float32) * scaling
        k = dot(gx, weight[1, :, cut])
        v = dot(gx, weight[2, :, cut])
        gq[2 * j] = jnp.where(glow, q, 0.0).astype(jnp.bfloat16)
        gq[2 * j + 1] = jnp.where(glow, swap_halves(q), 0.0).astype(jnp.bfloat16)
        gkv[2 * j] = jnp.where(glow, k, swap_halves(v)).astype(jnp.bfloat16)
        gkv[2 * j + 1] = jnp.where(glow, swap_halves(k), v).astype(jnp.bfloat16)

    for h in range(heads):
        keys = jnp.concatenate([kvb[b * heads + h] for b in range(blocks)], axis=0)
        s = dot_t(gq[h], keys)
        high = jnp.max(s, axis=-1, keepdims=True)
        e = jnp.exp(s - high)
        total = jnp.sum(e, axis=-1, keepdims=True)
        e_high = e.astype(jnp.bfloat16)
        e_low = (e - e_high.astype(jnp.float32)).astype(jnp.bfloat16)
        acc = dot(e_high, keys) + dot(e_low, keys)
        part[h * rows : (h + 1) * rows] = jnp.where(
            glane < HD // 2, high, jnp.where(glow, total, acc)
        )
    each_peer(lambda d: guarded(part_parts, d, lambda: part_copy(d, me).start()))

    to_right.wait_recv()
    to_left.wait_recv()
    win[0:heads] = halo_l[...]
    win[heads : heads + blocks * heads] = kvb[...]
    win[heads + blocks * heads :] = halo_r[...]

    def combine():
        part_in[me] = part[pl.ds(pl.multiple_of(me * rows_per, 8), rows_per)]
        each_peer(lambda d: part_copy(d, d).wait_recv())

        def top(d, best):
            return jnp.maximum(best, part_in[d])

        best = lax.fori_loop(1, n, top, part_in[0])[:, 0:1]

        def add(d, so_far):
            piece = part_in[d]
            return so_far + piece * jnp.exp(piece[:, 0:1] - best)

        summed = lax.fori_loop(0, n, add, jnp.zeros((rows_per, LANES), jnp.float32))
        done = summed / summed[:, HD // 2 : HD // 2 + 1]
        gmine[...] = done
        gout[pl.ds(pl.multiple_of(me * rows_per, 8), rows_per)] = done
        each_peer(lambda d: gout_copy(d, me).start())

    guarded(part_parts, me, combine)

    each_peer(lambda d: rand_copy(d, d).wait_recv())

    slots = 3 + R + g_count
    slot_lane = lax.broadcasted_iota(jnp.int32, (BS, slots * BS), 1)

    def block_step(b, carry):
        first = me * blocks + b
        start = jnp.where(first == 0, BS, 0)
        stop = jnp.where(first == n * blocks - 1, 2 * BS, 3 * BS)
        outside = (slot_lane < start) | ((slot_lane >= stop) & (slot_lane < 3 * BS))
        for j in range(pairs):
            halves = []
            for h in (2 * j, 2 * j + 1):
                at = b * heads + h
                keys = jnp.concatenate(
                    [win[at + t * heads] for t in range(3)]
                    + [rr[slot[at * R + r]] for r in range(R)]
                    + [gkv[h]],
                    axis=0,
                )
                s = jnp.where(outside, NEGATIVE, dot_t(qpad[at], keys))
                e = jnp.exp(s - jnp.max(s, axis=-1, keepdims=True))
                w = (e * (1.0 / jnp.sum(e, axis=-1, keepdims=True))).astype(jnp.bfloat16)
                halves.append(dot(w, keys))
            att[j, pl.ds(pl.multiple_of(b * BS, BS), BS), :] = jnp.where(
                low, swap_halves(halves[0]), halves[1]
            ).astype(jnp.bfloat16)
        return carry

    lax.fori_loop(0, blocks, block_step, 0)

    each_peer(lambda d: guarded(part_parts, d, lambda: gout_copy(d, d).wait_recv()))
    for j in range(pairs):
        for g in range(g_count):
            lo = (2 * j * g_count + g) * BS
            hi = ((2 * j + 1) * g_count + g) * BS
            row = jnp.where(low, swap_halves(gout[lo : lo + BS]), gout[hi : hi + BS])
            row = row.astype(jnp.bfloat16).astype(jnp.float32)
            for b in range(blocks):
                here = gids[g] == me * blocks + b
                old = att[j, b * BS : (b + 1) * BS, :].astype(jnp.float32)
                att[j, b * BS : (b + 1) * BS, :] = jnp.where(here, row, old).astype(jnp.bfloat16)

    def drain(d):
        tab_copy(d, me).wait_send()
        guarded(cand_parts, d, lambda: cand_copy(d, me).wait_send())
        guarded(cand_parts, me, lambda: gath_copy(d, me).wait_send())
        rand_copy(d, me).wait_send()
        guarded(part_parts, d, lambda: part_copy(d, me).wait_send())
        guarded(part_parts, me, lambda: gout_copy(d, me).wait_send())

    each_peer(drain)
    to_right.wait_send()
    to_left.wait_send()


def tail_kernel(
    chunks,
    att,
    states,
    out_w,
    up_w,
    down_w,
    gain1,
    gain2,
    out,
    mine1,
    theirs1,
    mine2,
    theirs2,
    s1,
    r1,
    s2,
    r2,
    normed,
):
    other = 1 - lax.axis_index("mp")
    barrier = pltpu.get_barrier_semaphore()
    pl.semaphore_signal(barrier, inc=1, device_id={"mp": other}, device_id_type=MESH)
    pl.semaphore_wait(barrier, 1)
    rows = states.shape[0] // chunks

    def swap(mine, theirs, ssem, rsem, c):
        return pltpu.make_async_remote_copy(
            src_ref=mine.at[c],
            dst_ref=theirs.at[c],
            send_sem=ssem.at[c],
            recv_sem=rsem.at[c],
            device_id={"mp": other},
            device_id_type=MESH,
        )

    for c in range(chunks):
        cut = slice(c * rows, (c + 1) * rows)
        acc = dot(att[0, cut, :], out_w[0:LANES, :])
        for j in range(1, att.shape[0]):
            acc = acc + dot(att[j, cut, :], out_w[j * LANES : (j + 1) * LANES, :])
        mine1[c] = acc.astype(mine1.dtype)
        swap(mine1, theirs1, s1, r1, c).start()
    for c in range(chunks):
        cut = slice(c * rows, (c + 1) * rows)
        swap(mine1, theirs1, s1, r1, c).wait_recv()
        summed = mine1[c].astype(jnp.float32) + theirs1[c].astype(jnp.float32)
        norm = layer_norm(states[cut, :].astype(jnp.float32) + summed, gain1[...])
        norm = norm.astype(jnp.bfloat16)
        normed[c] = norm
        v = dot(norm, up_w[...])
        hidden = (v * (1.0 + lax.erf(v * (0.5**0.5))) * 0.5).astype(jnp.bfloat16)
        mine2[c] = dot(hidden, down_w[...]).astype(mine2.dtype)
        swap(mine2, theirs2, s2, r2, c).start()
    for c in range(chunks):
        cut = slice(c * rows, (c + 1) * rows)
        swap(mine2, theirs2, s2, r2, c).wait_recv()
        summed = mine2[c].astype(jnp.float32) + theirs2[c].astype(jnp.float32)
        out[cut, :] = layer_norm(normed[c].astype(jnp.float32) + summed, gain2[...]).astype(
            jnp.bfloat16
        )
    for c in range(chunks):
        swap(mine1, theirs1, s1, r1, c).wait_send()
        swap(mine2, theirs2, s2, r2, c).wait_send()


def vmem_specs(count):
    return [pl.BlockSpec(memory_space=pltpu.VMEM)] * count


def shards(
    states,
    qkv_weight,
    out_weight,
    up_weight,
    down_weight,
    attn_gain,
    mlp_gain,
    global_ids,
    random_owner,
    random_local,
):
    tokens, width = states.shape
    heads = qkv_weight.shape[2] // HD
    pairs = heads // 2
    blocks = tokens // BS
    g_count = global_ids.shape[0]
    n = lax.axis_size("seq")

    owner = random_owner.reshape(-1)
    items = owner.shape[0]
    cap = max(2, items // n + 1)
    head_list = jnp.broadcast_to(
        jnp.arange(heads, dtype=jnp.int32)[None, :, None], (blocks, heads, R)
    ).reshape(-1)
    code = random_local.reshape(-1) * heads + head_list
    earlier = jnp.arange(items)[:, None] > jnp.arange(items)[None, :]
    rank = jnp.sum(((owner[:, None] == owner[None, :]) & earlier).astype(jnp.int32), axis=1)
    slot = owner * cap + rank
    place = owner * LANES + rank
    wanted = jnp.sum(
        jnp.where(
            place[None, None, :]
            == (jnp.arange(n)[:, None] * LANES + jnp.arange(LANES)[None, :])[:, :, None],
            code[None, None, :],
            0,
        ),
        axis=2,
    ).reshape(n, 1, LANES)

    units = g_count * (width // LANES) * (BS // 16)
    per = max(1, units // n)
    part_rows = heads * g_count * BS
    rows_per = -(-part_rows // n // 8) * 8
    bf, f32 = jnp.bfloat16, jnp.float32
    own = blocks * heads
    dma = pltpu.SemaphoreType.DMA
    att = pl.pallas_call(
        functools.partial(attend_kernel, n, cap, heads, blocks, g_count),
        out_shape=jax.ShapeDtypeStruct((pairs, tokens, LANES), bf),
        in_specs=vmem_specs(3) + [pl.BlockSpec(memory_space=pltpu.SMEM)] * 2,
        out_specs=pl.BlockSpec(memory_space=pltpu.VMEM),
        scratch_shapes=[
            pltpu.VMEM((n, 1, LANES), jnp.int32),
            pltpu.SMEM((n, 1, LANES), jnp.int32),
            pltpu.VMEM((units, 16, LANES), bf),
            pltpu.VMEM((n, per, 16, LANES), bf),
            pltpu.VMEM((per, 16, LANES), bf),
            pltpu.VMEM((units, 16, LANES), bf),
            pltpu.VMEM((g_count * BS, width), bf),
            pltpu.VMEM((own, BS, LANES), bf),
            pltpu.VMEM((own, BS, LANES), bf),
            pltpu.VMEM((n * cap, BS, LANES), bf),
            pltpu.VMEM((n * cap, BS, LANES), bf),
            pltpu.VMEM((heads, BS, LANES), bf),
            pltpu.VMEM((heads, BS, LANES), bf),
            pltpu.VMEM((own + 2 * heads, BS, LANES), bf),
            pltpu.VMEM((heads, g_count * BS, LANES), bf),
            pltpu.VMEM((heads, g_count * BS, LANES), bf),
            pltpu.VMEM((part_rows, LANES), f32),
            pltpu.VMEM((n, rows_per, LANES), f32),
            pltpu.VMEM((rows_per, LANES), f32),
            pltpu.VMEM((part_rows, LANES), f32),
        ]
        + [dma((n,))] * 8
        + [dma((2,))] * 2
        + [dma((n,))] * 4
        + [dma(())],
        compiler_params=pltpu.CompilerParams(
            collective_id=0, has_side_effects=True, vmem_limit_bytes=32 * 1024 * 1024
        ),
    )(states, qkv_weight, wanted, slot, global_ids)

    chunks = 4
    rows = tokens // chunks
    link = jnp.bfloat16
    return pl.pallas_call(
        functools.partial(tail_kernel, chunks),
        out_shape=jax.ShapeDtypeStruct((tokens, width), bf),
        in_specs=vmem_specs(7),
        out_specs=pl.BlockSpec(memory_space=pltpu.VMEM),
        scratch_shapes=[pltpu.VMEM((chunks, rows, width), link)] * 4
        + [dma((chunks,))] * 4
        + [pltpu.VMEM((chunks, rows, width), bf)],
        compiler_params=pltpu.CompilerParams(
            collective_id=1, has_side_effects=True, vmem_limit_bytes=32 * 1024 * 1024
        ),
    )(
        att,
        states,
        out_weight,
        up_weight,
        down_weight,
        attn_gain.reshape(1, width),
        mlp_gain.reshape(1, width),
    )


def solution(mesh):
    in_specs = (
        P("seq", None),
        P(None, None, "mp"),
        P("mp", None),
        P(None, "mp"),
        P("mp", None),
        P(),
        P(),
        P(),
        P("mp", "seq", None, None),
        P("mp", "seq", None, None),
    )
    out_specs = P("seq", None)
    return jax.shard_map(shards, mesh=mesh, in_specs=in_specs, out_specs=out_specs, check_vma=False)
```

time: 397 us -> 91.4 us (0.23)
  blocking collectives: 164 us -> 0 us
  Pallas kernels: 0 us -> 80.6 us
  waiting for transfers between devices: 68 us -> 0 us
  other arithmetic: 57.4 us -> 1.09 us
  local copies, waits for them, and re-layouts: 44.7 us -> 9.33 us
  matrix products: 29.3 us -> 0 us
  starting transfers between devices: 15.6 us -> 0 us
  between operations: 13.7 us -> 0.09 us
    all_gather x2 -> x0, blocking collectives: 87 us -> none  [merged(): pieces = jax.tree.map(lambda part: lax.all_gather(part, axis), value)]
    pallas_call x0 -> x2, Pallas kernels: none -> 80.6 us  [the longest x1 68.7 us: shards(): pl.pallas_call(functools.partial(attend_kernel, n, cap, heads, blocks, g_...]
    psum x1 -> x0, blocking collectives: 68.3 us -> none  [shards(): summed_query, summed_pair = lax.psum((local_query, local_pair), 'seq')]
    psum x2 -> x0, waiting for transfers between devices: 68 us -> none  [the longest x1 47.7 us: shards(): lax.psum(jnp.dot(attended, out_weight, preferred_element_type=jnp.float32...]
    add x33 -> x3, other arithmetic: 32.7 us -> 0.08 us  [the longest x1 0.07 us: shards(): jnp.arange(n)[:, None] * LANES + jnp.arange(LANES)[None, :]]
    dot_general x13 -> x0, matrix products: 28.9 us -> none  [the longest x1 7.16 us: shards(): jnp.dot(hidden, down_weight, preferred_element_type=jnp.float32)]
    concatenate x8 -> x0, local copies, waits for them, and re-layouts: 11.4 us -> none  [shards(): jnp.concatenate([key_part.reshape(tokens_here, head_count, HD), value_par...]
    all_to_all x1 -> x0, blocking collectives: 9.2 us -> none  [shards(): lax.all_to_all(wanted, 'seq', split_axis=0, concat_axis=0, tiled=True)]
  transfers between devices with their start and end apart: 6 -> 0, of which waited for: 2 -> 0; matrix products, arithmetic and copies ran while one was open for 13% -> 0% of each run, Pallas kernels for 0% -> 0%
where the time goes in v1:
time: 91.4 us; the launch traced here: 91.1 us
  Pallas kernels  80.6 us (88%)
  local copies, waits for them, and re-layouts  9.33 us (10%)
  other arithmetic  1.09 us (1%)
    pallas_call x1, Pallas kernels, shards(): pl.pallas_call(functools.partial(attend_kernel, n, cap, heads, blocks, g_...  68.7 us
    pallas_call x1, Pallas kernels, shards(): pl.pallas_call(functools.partial(tail_kernel, chunks), out_shape=jax.Shap...  11.9 us
    unnamed x14, local copies, waits for them, and re-layouts  7.4 us

profile of v1, /device:TPU:31, one launch (start us, length us, event | category | flops | bytes accessed | tf_op | source)
XLA Modules:
  0.0 91.1 jit_solution(13748408528291640665)
XLA Ops:
  0.0 0.0 copy-start
  0.0 0.8 reshape.66.gain1
  0.8 0.7 reshape.67.gain2
  1.5 0.7 broadcast_multiply_fusion
  2.2 0.1 iota_add_fusion
  2.3 0.1 copy.16
  2.4 0.1 mul.42
  2.5 0.8 copy.15
  3.3 0.1 reshape.63
  3.4 0.2 convert_reduce_fusion
  3.6 0.1 reshape.64
  3.7 0.1 select_reduce_fusion
  3.9 0.0 copy-start.2
  3.9 1.5 %copy-done.2 = bf16[3,768,384]{2,1,0:T(8,128)(2,1)S(1)} copy-done((bf16[3,768,384]{2,1,0:T(8,128)(2,1)S(1)}, bf16[3,768,384]{2,1,0:T(8,128)(2,1)}, u32[]{:S(2)}) %copy-start.2) | copy-done | bytes 1769496
  5.3 0.0 copy-start.3
  5.3 1.0 %copy-done.3 = bf16[256,768]{1,0:T(8,128)(2,1)S(1)} copy-done((bf16[256,768]{1,0:T(8,128)(2,1)S(1)}, bf16[256,768]{1,0:T(8,128)(2,1)}, u32[]{:S(2)}) %copy-start.3) | copy-done | bytes 393240
  6.3 0.7 copy-done.5
  7.0 68.7 %shard_map.100.att = bf16[3,256,128]{2,1,0:T(8,128)(2,1)S(1)} custom-call(bf16[256,768]{1,0:T(8,128)(2,1)S(1)} %copy-done.3, bf16[3,768,384]{2,1,0:T(8,128)(2,1)S(1)} %copy-done.2, s32[16,1,128]{2,1,0:T(1,128)S(1)} %bitcast.1, s32[72]{0:T(128)S(1)} %get-tuple-element.5.slot, s32[2]{0:T(128)S(1)} %copy-done.5), custom_call_target="tpu_custom_call" | custom-call | tf_op jit(solution)/shard_map/pallas_call | solution.py:485
  75.7 0.0 copy-done
  75.7 0.0 copy-start.1
  75.7 1.7 %copy-done.1 = bf16[1536,768]{1,0:T(8,128)(2,1)S(1)} copy-done((bf16[1536,768]{1,0:T(8,128)(2,1)S(1)}, bf16[1536,768]{1,0:T(8,128)(2,1)}, u32[]{:S(2)}) %copy-start.1) | copy-done | bytes 2359320
  77.4 1.1 %copy-done.4 = bf16[384,768]{1,0:T(8,128)(2,1)S(1)} copy-done((bf16[384,768]{1,0:T(8,128)(2,1)S(1)}, bf16[384,768]{1,0:T(8,128)(2,1)}, u32[]{:S(2)}) %copy-start.4) | copy-done | bytes 589848
  78.4 11.9 %shard_map.101 = bf16[256,768]{1,0:T(8,128)(2,1)S(1)} custom-call(bf16[3,256,128]{2,1,0:T(8,128)(2,1)S(1)} %shard_map.100.att, bf16[256,768]{1,0:T(8,128)(2,1)S(1)} %copy-done.3, bf16[384,768]{1,0:T(8,128)(2,1)S(1)} %copy-done.4, bf16[768,1536]{1,0:T(8,128)(2,1)S(1)} %copy-done, bf16[1536,768]{1,0:T(8,128)(2,1)S(1)} %copy-done.1, ...), custom_call_target="tpu_custom_call" | custom-call | tf_op jit(solution)/shard_map/pallas_call | solution.py:524
  90.3 0.7 copy.18
  (6 shorter events, 0.0 us)
Async XLA Ops:
  0.0 75.7 %copy-start = (bf16[768,1536]{1,0:T(8,128)(2,1)S(1)}, bf16[768,1536]{1,0:T(8,128)(2,1)}, u32[]{:S(2)}) copy-start(bf16[768,1536]{1,0:T(8,128)(2,1)} %up_w.1) | copy-start | bytes 7077892
  3.9 1.5 %copy-start.2 = (bf16[3,768,384]{2,1,0:T(8,128)(2,1)S(1)}, bf16[3,768,384]{2,1,0:T(8,128)(2,1)}, u32[]{:S(2)}) copy-start(bf16[3,768,384]{2,1,0:T(8,128)(2,1)} %weight.1) | copy-start | bytes 5308420
  5.3 1.0 %copy-start.3 = (bf16[256,768]{1,0:T(8,128)(2,1)S(1)}, bf16[256,768]{1,0:T(8,128)(2,1)}, u32[]{:S(2)}) copy-start(bf16[256,768]{1,0:T(8,128)(2,1)} %states.3) | copy-start | bytes 1179652
  6.3 0.7 copy-start.5
  75.7 1.7 %copy-start.1 = (bf16[1536,768]{1,0:T(8,128)(2,1)S(1)}, bf16[1536,768]{1,0:T(8,128)(2,1)}, u32[]{:S(2)}) copy-start(bf16[1536,768]{1,0:T(8,128)(2,1)} %down_w.1) | copy-start | bytes 7077892
  77.4 1.1 %copy-start.4 = (bf16[384,768]{1,0:T(8,128)(2,1)S(1)}, bf16[384,768]{1,0:T(8,128)(2,1)}, u32[]{:S(2)}) copy-start(bf16[384,768]{1,0:T(8,128)(2,1)} %out_w.1) | copy-start | bytes 1769476

commit v2 on v1

--- a/solution.py
+++ b/solution.py
@@ -42,12 +42,14 @@
     heads,
     blocks,
     g_count,
-    states,
-    weight,
+    states_hbm,
+    weight_hbm,
     wanted,
     slot,
     gids,
     att,
+    states,
+    weight,
     tab,
     tab_s,
     cand,
@@ -82,18 +84,24 @@
     r_part,
     s_gout,
     r_gout,
+    s_mp,
+    r_mp,
     l_sem,
+    w_sem,
 ):
     me = lax.axis_index("seq")
+    mine = lax.axis_index("mp")
     pairs = heads // 2
     width = states.shape[1]
     cols = width // LANES
     quarters = BS // 16
-    units = g_count * cols * quarters
+    half = gath.shape[0]
+    gper = gath.shape[1] // (cols * quarters)
+    units = gper * cols * quarters
     per = cand_in.shape[1]
     cand_parts = units // per
-    rows_per = part_in.shape[1]
-    part_parts = part.shape[0] // rows_per
+    rows_per = part_in.shape[2]
+    part_parts = part.shape[0]
     left = lax.rem(me + n - 1, n)
     right = lax.rem(me + 1, n)
 
@@ -126,14 +134,14 @@
     def tab_copy(d, owner):
         return remote(wanted.at[d], tab.at[owner], s_tab.at[d], r_tab.at[owner], d)
 
-    def cand_copy(d, owner):
+    def cand_copy(d, owner, at):
         return remote(
-            cand.at[pl.ds(d * per, per)], cand_in.at[owner], s_cand.at[d], r_cand.at[owner], d
+            cand.at[pl.ds(at * per, per)], cand_in.at[owner], s_cand.at[d], r_cand.at[owner], d
         )
 
     def gath_copy(d, owner):
         return remote(
-            pick, gath.at[pl.ds(owner * per, per)], s_gath.at[d], r_gath.at[owner], d
+            pick, gath.at[mine, pl.ds(owner * per, per)], s_gath.at[d], r_gath.at[owner], d
         )
 
     def rand_copy(d, owner):
@@ -145,22 +153,21 @@
             d,
         )
 
-    def part_copy(d, owner):
-        return remote(
-            part.at[pl.ds(pl.multiple_of(d * rows_per, 8), rows_per)],
-            part_in.at[owner],
-            s_part.at[d],
-            r_part.at[owner],
-            d,
-        )
+    def part_copy(d, owner, at):
+        return remote(part.at[at], part_in.at[owner], s_part.at[d], r_part.at[owner], d)
 
     def gout_copy(d, owner):
-        return remote(
-            gmine,
-            gout.at[pl.ds(pl.multiple_of(owner * rows_per, 8), rows_per)],
-            s_gout.at[d],
-            r_gout.at[owner],
-            d,
+        return remote(gmine, gout.at[owner], s_gout.at[d], r_gout.at[owner], d)
+
+    def mp_copy(k, owner):
+        other = lax.rem(mine + k, half)
+        return pltpu.make_async_remote_copy(
+            src_ref=gath.at[mine],
+            dst_ref=gath.at[owner],
+            send_sem=s_mp.at[k],
+            recv_sem=r_mp.at[owner],
+            device_id={"mp": other},
+            device_id_type=MESH,
         )
 
     to_right = remote(
@@ -168,30 +175,39 @@
     )
     to_left = remote(kvb.at[pl.ds(0, heads)], halo_r, s_halo.at[1], r_halo.at[1], left)
 
-    for g in range(g_count):
-        local = lax.rem(gids[g], blocks)
+    loads = [pltpu.make_async_copy(states_hbm, states, w_sem.at[3])] + [
+        pltpu.make_async_copy(weight_hbm.at[i], weight.at[i], w_sem.at[i]) for i in (1, 2, 0)
+    ]
+    for load in loads:
+        load.start()
+
+    barrier = pltpu.get_barrier_semaphore()
+    each_peer(
+        lambda d: pl.semaphore_signal(barrier, inc=1, device_id={"seq": d}, device_id_type=MESH)
+    )
+    for k in range(1, half):
+        pl.semaphore_signal(
+            barrier, inc=1, device_id={"mp": lax.rem(mine + k, half)}, device_id_type=MESH
+        )
+
+    loads[0].wait()
+    for i in range(gper):
+        local = lax.rem(gids[mine * gper + i], blocks)
         for j in range(cols):
             cut = slice(j * LANES, (j + 1) * LANES)
             piece = states[0:BS, cut]
             for b in range(1, blocks):
                 piece = jnp.where(local == b, states[b * BS : (b + 1) * BS, cut], piece)
             for q in range(quarters):
-                cand[(g * cols + j) * quarters + q] = piece[q * 16 : (q + 1) * 16]
-
-    barrier = pltpu.get_barrier_semaphore()
-    each_peer(
-        lambda d: pl.semaphore_signal(barrier, inc=1, device_id={"seq": d}, device_id_type=MESH)
-    )
-    pl.semaphore_wait(barrier, n - 1)
-
-    each_peer(lambda d: tab_copy(d, me).start())
-    each_peer(lambda d: guarded(cand_parts, d, lambda: cand_copy(d, me).start()))
+                cand[(i * cols + j) * quarters + q] = piece[q * 16 : (q + 1) * 16]
     tab[me] = wanted[me]
 
     def own_cand():
         cand_in[me] = cand[pl.ds(me * per, per)]
 
     guarded(cand_parts, me, own_cand)
+    loads[1].wait()
+    loads[2].wait()
 
     lane = lax.broadcasted_iota(jnp.int32, (BS, LANES), 1)
     low = lane < HD
@@ -205,39 +221,13 @@
             kvb[b * heads + 2 * j] = jnp.where(low, kb, swap_halves(vb)).astype(jnp.bfloat16)
             kvb[b * heads + 2 * j + 1] = jnp.where(low, swap_halves(kb), vb).astype(jnp.bfloat16)
 
+    pl.semaphore_wait(barrier, n - 1 + half - 1)
+    each_peer(lambda d: tab_copy(d, me).start())
+    each_peer(lambda d: guarded(cand_parts, d, lambda: cand_copy(d, me, d).start()))
     to_right.start()
     to_left.start()
 
-    each_peer(lambda d: tab_copy(d, d).wait_recv())
-    table = pltpu.make_async_copy(tab, tab_s, l_sem)
-    table.start()
-    table.wait()
-
-    def serve(d):
-        for c in range(cap):
-            stage[d * cap + c] = kvb[tab_s[d, 0, c]]
-        rand_copy(d, me).start()
-
-    each_peer(serve)
-    for c in range(cap):
-        rr[me * cap + c] = kvb[tab_s[me, 0, c]]
-
-    def relay():
-        each_peer(lambda d: cand_copy(d, d).wait_recv())
-        for u in range(per):
-            g = (me * per + u) // (cols * quarters)
-            wanted_id = gids[g]
-
-            def choose(d, so_far):
-                here = (wanted_id >= d * blocks) & (wanted_id < (d + 1) * blocks)
-                return jnp.where(here, cand_in[d, u], so_far)
-
-            pick[u] = lax.fori_loop(1, n, choose, cand_in[0, u])
-        gath[pl.ds(me * per, per)] = pick[...]
-        each_peer(lambda d: gath_copy(d, me).start())
-
-    guarded(cand_parts, me, relay)
-
+    loads[3].wait()
     scaling = HD ** (-0.5)
     for j in range(pairs):
         cut = slice(j * LANES, (j + 1) * LANES)
@@ -247,12 +237,54 @@
             qpad[b * heads + 2 * j] = jnp.where(low, qb, 0.0).astype(jnp.bfloat16)
             qpad[b * heads + 2 * j + 1] = jnp.where(low, swap_halves(qb), 0.0).astype(jnp.bfloat16)
 
+    each_peer(lambda d: tab_copy(d, d).wait_recv())
+    table = pltpu.make_async_copy(tab, tab_s, l_sem)
+    table.start()
+    table.wait()
+
+    def serve(d):
+        for c in range(cap):
+            stage[d * cap + c] = kvb[tab_s[d, 0, c]]
+        rand_copy(d, me).start()
+
+    def serve_some(start, stop):
+        def step(k, carry):
+            serve(peer(k))
+            return carry
+
+        lax.fori_loop(start, stop, step, 0)
+
+    batch = 1 + n // 3
+    serve_some(1, batch)
+    for c in range(cap):
+        rr[me * cap + c] = kvb[tab_s[me, 0, c]]
+
+    def relay():
+        each_peer(lambda d: cand_copy(d, d, me).wait_recv())
+        for u in range(per):
+            g = (me * per + u) // (cols * quarters)
+            wanted_id = gids[mine * gper + g]
+
+            def choose(d, so_far):
+                here = (wanted_id >= d * blocks) & (wanted_id < (d + 1) * blocks)
+                return jnp.where(here, cand_in[d, u], so_far)
+
+            pick[u] = lax.fori_loop(1, n, choose, cand_in[0, u])
+        gath[mine, pl.ds(me * per, per)] = pick[...]
+        each_peer(lambda d: gath_copy(d, me).start())
+
+    guarded(cand_parts, me, relay)
+
     each_peer(lambda d: guarded(cand_parts, d, lambda: gath_copy(d, d).wait_recv()))
+    for k in range(1, half):
+        mp_copy(k, mine).start()
+    for k in range(1, half):
+        mp_copy(k, lax.rem(mine + k, half)).wait_recv()
     for g in range(g_count):
         for j in range(cols):
             for q in range(quarters):
                 gstates[g * BS + q * 16 : g * BS + (q + 1) * 16, j * LANES : (j + 1) * LANES] = (
-                    gath[(g * cols + j) * quarters + q]
+                    gath[g // gper, ((g % gper) * cols + j) * quarters + q]
                 )
     gx = gstates[...]
     rows = g_count * BS
@@ -276,11 +308,21 @@
         total = jnp.sum(e, axis=-1, keepdims=True)
         e_high = e.astype(jnp.bfloat16)
         e_low = (e - e_high.astype(jnp.float32)).astype(jnp.bfloat16)
-        acc = dot(e_high, keys) + dot(e_low, keys)
-        part[h * rows : (h + 1) * rows] = jnp.where(
-            glane < HD // 2, high, jnp.where(glow, total, acc)
-        )
-    each_peer(lambda d: guarded(part_parts, d, lambda: part_copy(d, me).start()))
+        acc = (dot(e_high, keys) + dot(e_low, keys)) * (1.0 / total)
+        level = high + jnp.log(total)
+        first = level.astype(jnp.bfloat16).astype(jnp.float32)
+        second = (level - first).astype(jnp.bfloat16).astype(jnp.float32)
+        third = level - first - second
+        packed = jnp.where(
+            glane < 16,
+            first,
+            jnp.where(glane < 32, second, jnp.where(glow, third, acc)),
+        ).astype(jnp.bfloat16)
+        cuts = rows // rows_per
+        for c in range(cuts):
+            part[(h // 2) * cuts + c, h % 2] = packed[c * rows_per : (c + 1) * rows_per]
+    each_peer(lambda d: guarded(part_parts, d, lambda: part_copy(d, me, d).start()))
+    serve_some(batch, n)
 
     to_right.wait_recv()
     to_left.wait_recv()
@@ -289,22 +331,32 @@
     win[heads + blocks * heads :] = halo_r[...]
 
     def combine():
-        part_in[me] = part[pl.ds(pl.multiple_of(me * rows_per, 8), rows_per)]
-        each_peer(lambda d: part_copy(d, d).wait_recv())
-
-        def top(d, best):
-            return jnp.maximum(best, part_in[d])
-
-        best = lax.fori_loop(1, n, top, part_in[0])[:, 0:1]
-
-        def add(d, so_far):
-            piece = part_in[d]
-            return so_far + piece * jnp.exp(piece[:, 0:1] - best)
-
-        summed = lax.fori_loop(0, n, add, jnp.zeros((rows_per, LANES), jnp.float32))
-        done = summed / summed[:, HD // 2 : HD // 2 + 1]
+        part_in[me] = part[me]
+        each_peer(lambda d: part_copy(d, d, me).wait_recv())
+        outs = []
+        for parity in range(2):
+
+            def level(d):
+                piece = part_in[d, parity].astype(jnp.float32)
+                return piece, piece[:, 0:1] + piece[:, 16:17] + piece[:, 32:33]
+
+            def top(d, best):
+                return jnp.maximum(best, level(d)[1])
+
+            best = lax.fori_loop(1, n, top, level(0)[1])
+
+            def add(d, so_far):
+                piece, high = level(d)
+                factor = jnp.exp(high - best)
+                return so_far[0] + piece * factor, so_far[1] + factor
+
+            zero = (jnp.zeros((rows_per, LANES), jnp.float32), jnp.zeros((rows_per, 1), jnp.float32))
+            summed, total = lax.fori_loop(0, n, add, zero)
+            outs.append(summed / total)
+        plow = lax.broadcasted_iota(jnp.int32, (rows_per, LANES), 1) < HD
+        done = jnp.where(plow, swap_halves(outs[0]), outs[1]).astype(jnp.bfloat16)
         gmine[...] = done
-        gout[pl.ds(pl.multiple_of(me * rows_per, 8), rows_per)] = done
+        gout[me] = done
         each_peer(lambda d: gout_copy(d, me).start())
 
     guarded(part_parts, me, combine)
@@ -343,10 +395,9 @@
     each_peer(lambda d: guarded(part_parts, d, lambda: gout_copy(d, d).wait_recv()))
     for j in range(pairs):
         for g in range(g_count):
-            lo = (2 * j * g_count + g) * BS
-            hi = ((2 * j + 1) * g_count + g) * BS
-            row = jnp.where(low, swap_halves(gout[lo : lo + BS]), gout[hi : hi + BS])
-            row = row.astype(jnp.bfloat16).astype(jnp.float32)
+            cuts = BS // rows_per
+            at = (j * g_count + g) * cuts
+            row = jnp.concatenate([gout[at + c] for c in range(cuts)], axis=0).astype(jnp.float32)
             for b in range(blocks):
                 here = gids[g] == me * blocks + b
                 old = att[j, b * BS : (b + 1) * BS, :].astype(jnp.float32)
@@ -354,13 +405,15 @@
 
     def drain(d):
         tab_copy(d, me).wait_send()
-        guarded(cand_parts, d, lambda: cand_copy(d, me).wait_send())
+        guarded(cand_parts, d, lambda: cand_copy(d, me, d).wait_send())
         guarded(cand_parts, me, lambda: gath_copy(d, me).wait_send())
         rand_copy(d, me).wait_send()
-        guarded(part_parts, d, lambda: part_copy(d, me).wait_send())
+        guarded(part_parts, d, lambda: part_copy(d, me, d).wait_send())
         guarded(part_parts, me, lambda: gout_copy(d, me).wait_send())
 
     each_peer(drain)
+    for k in range(1, half):
+        mp_copy(k, mine).wait_send()
     to_right.wait_send()
     to_left.wait_send()
 
@@ -475,25 +528,31 @@
         axis=2,
     ).reshape(n, 1, LANES)
 
-    units = g_count * (width // LANES) * (BS // 16)
-    per = max(1, units // n)
-    part_rows = heads * g_count * BS
-    rows_per = -(-part_rows // n // 8) * 8
-    bf, f32 = jnp.bfloat16, jnp.float32
+    half = lax.axis_size("mp")
+    units = (g_count // half) * (width // LANES) * (BS // 16)
+    per = -(-units // n)
+    part_rows = pairs * g_count * BS
+    rows_per = -(-part_rows // n // 16) * 16
+    parts = part_rows // rows_per
+    bf = jnp.bfloat16
     own = blocks * heads
     dma = pltpu.SemaphoreType.DMA
     att = pl.pallas_call(
         functools.partial(attend_kernel, n, cap, heads, blocks, g_count),
         out_shape=jax.ShapeDtypeStruct((pairs, tokens, LANES), bf),
-        in_specs=vmem_specs(3) + [pl.BlockSpec(memory_space=pltpu.SMEM)] * 2,
+        in_specs=[pl.BlockSpec(memory_space=pltpu.HBM)] * 2
+        + vmem_specs(1)
+        + [pl.BlockSpec(memory_space=pltpu.SMEM)] * 2,
         out_specs=pl.BlockSpec(memory_space=pltpu.VMEM),
         scratch_shapes=[
+            pltpu.VMEM((tokens, width), bf),
+            pltpu.VMEM(qkv_weight.shape, bf),
             pltpu.VMEM((n, 1, LANES), jnp.int32),
             pltpu.SMEM((n, 1, LANES), jnp.int32),
             pltpu.VMEM((units, 16, LANES), bf),
             pltpu.VMEM((n, per, 16, LANES), bf),
             pltpu.VMEM((per, 16, LANES), bf),
-            pltpu.VMEM((units, 16, LANES), bf),
+            pltpu.VMEM((half, units, 16, LANES), bf),
             pltpu.VMEM((g_count * BS, width), bf),
             pltpu.VMEM((own, BS, LANES), bf),
             pltpu.VMEM((own, BS, LANES), bf),
@@ -504,19 +563,29 @@
             pltpu.VMEM((own + 2 * heads, BS, LANES), bf),
             pltpu.VMEM((heads, g_count * BS, LANES), bf),
             pltpu.VMEM((heads, g_count * BS, LANES), bf),
-            pltpu.VMEM((part_rows, LANES), f32),
-            pltpu.VMEM((n, rows_per, LANES), f32),
-            pltpu.VMEM((rows_per, LANES), f32),
-            pltpu.VMEM((part_rows, LANES), f32),
+            pltpu.VMEM((parts, 2, rows_per, LANES), bf),
+            pltpu.VMEM((n, 2, rows_per, LANES), bf),
+            pltpu.VMEM((rows_per, LANES), bf),
+            pltpu.VMEM((parts, rows_per, LANES), bf),
         ]
         + [dma((n,))] * 8
         + [dma((2,))] * 2
         + [dma((n,))] * 4
-        + [dma(())],
+        + [dma((half,))] * 2
+        + [dma(()), dma((4,))],
+        cost_estimate=pl.CostEstimate(
+            flops=30_000_000_000, bytes_accessed=20_000_000, transcendentals=0
+        ),
         compiler_params=pltpu.CompilerParams(
             collective_id=0, has_side_effects=True, vmem_limit_bytes=32 * 1024 * 1024
         ),
-    )(states, qkv_weight, wanted, slot, global_ids)
+    )(
+        pltpu.with_memory_space_constraint(states, pltpu.HBM),
+        pltpu.with_memory_space_constraint(qkv_weight, pltpu.HBM),
+        wanted,
+        slot,
+        global_ids,
+    )
 
     chunks = 4
     rows = tokens // chunks

time: 91.4 us -> 83.4 us (0.912)
  local copies, waits for them, and re-layouts: 9.33 us -> 3.99 us
  Pallas kernels: 80.6 us -> 77.1 us
    unnamed x14 -> x12, local copies, waits for them, and re-layouts: 7.4 us -> 2.21 us
    pallas_call x1, Pallas kernels: 11.9 us -> 8.44 us  [shards(): pl.pallas_call(functools.partial(tail_kernel, chunks), out_shape=jax.Shap...]
where the time goes in v2:
time: 83.4 us; the launch traced here: 82.3 us
  Pallas kernels  77.1 us (92%)
  local copies, waits for them, and re-layouts  3.99 us (5%)
  other arithmetic  1.09 us (1%)
    pallas_call x1, Pallas kernels, shards(): pl.pallas_call(functools.partial(attend_kernel, n, cap, heads, blocks, g_...  68.7 us
    pallas_call x1, Pallas kernels, shards(): pl.pallas_call(functools.partial(tail_kernel, chunks), out_shape=jax.Shap...  8.44 us
    unnamed x12, local copies, waits for them, and re-layouts  2.21 us

profile of v2, /device:TPU:31, one launch (start us, length us, event | category | flops | bytes accessed | tf_op | source)
XLA Modules:
  0.0 82.3 jit_solution(16596863899573315271)
XLA Ops:
  0.0 0.7 reshape.66.gain1
  0.7 0.7 reshape.67.gain2
  1.4 0.7 broadcast_multiply_fusion
  2.1 0.1 iota_add_fusion
  2.1 0.1 copy.16
  2.3 0.1 mul.42
  2.4 0.8 copy.15
  3.2 0.1 reshape.63
  3.3 0.2 convert_reduce_fusion
  3.5 0.1 reshape.64
  3.6 0.1 select_reduce_fusion
  3.7 0.0 copy-start.4
  3.7 0.6 copy-done.4
  4.4 0.0 copy-start
  4.4 0.0 copy-start.1
  4.4 0.0 copy-start.2
  4.4 0.0 copy-start.3
  4.4 68.7 %shard_map.100.att = bf16[3,256,128]{2,1,0:T(8,128)(2,1)S(1)} custom-call(bf16[256,768]{1,0:T(8,128)(2,1)} %states.1, bf16[3,768,384]{2,1,0:T(8,128)(2,1)} %weight_hbm.1, s32[16,1,128]{2,1,0:T(1,128)S(1)} %bitcast.1, s32[72]{0:T(128)S(1)} %get-tuple-element.5.slot, s32[2]{0:T(128)S(1)} %copy-done.4), custom_call_target="tpu_custom_call" | custom-call | flops 30000001024 | bytes 20000000 | tf_op jit(solution)/shard_map/pallas_call | solution.py:540
  73.1 0.0 copy-done
  73.1 0.0 copy-done.1
  73.1 0.0 copy-done.2
  73.1 0.0 copy-done.3
  73.1 8.4 %shard_map.101 = bf16[256,768]{1,0:T(8,128)(2,1)S(1)} custom-call(bf16[3,256,128]{2,1,0:T(8,128)(2,1)S(1)} %shard_map.100.att, bf16[256,768]{1,0:T(8,128)(2,1)S(1)} %copy-done.3, bf16[384,768]{1,0:T(8,128)(2,1)S(1)} %copy-done.2, bf16[768,1536]{1,0:T(8,128)(2,1)S(1)} %copy-done, bf16[1536,768]{1,0:T(8,128)(2,1)S(1)} %copy-done.1, ...), custom_call_target="tpu_custom_call" | custom-call | tf_op jit(solution)/shard_map/pallas_call | solution.py:593
  81.6 0.7 copy.18
  (4 shorter events, 0.0 us)
Async XLA Ops:
  3.7 0.7 copy-start.4
  4.4 68.7 %copy-start = (bf16[768,1536]{1,0:T(8,128)(2,1)S(1)}, bf16[768,1536]{1,0:T(8,128)(2,1)}, u32[]{:S(2)}) copy-start(bf16[768,1536]{1,0:T(8,128)(2,1)} %up_w.1) | copy-start | bytes 7077892
  4.4 68.7 %copy-start.1 = (bf16[1536,768]{1,0:T(8,128)(2,1)S(1)}, bf16[1536,768]{1,0:T(8,128)(2,1)}, u32[]{:S(2)}) copy-start(bf16[1536,768]{1,0:T(8,128)(2,1)} %down_w.1) | copy-start | bytes 7077892
  4.4 68.7 %copy-start.2 = (bf16[384,768]{1,0:T(8,128)(2,1)S(1)}, bf16[384,768]{1,0:T(8,128)(2,1)}, u32[]{:S(2)}) copy-start(bf16[384,768]{1,0:T(8,128)(2,1)} %out_w.1) | copy-start | bytes 1769476
  4.4 68.7 %copy-start.3 = (bf16[256,768]{1,0:T(8,128)(2,1)S(1)}, bf16[256,768]{1,0:T(8,128)(2,1)}, u32[]{:S(2)}) copy-start(bf16[256,768]{1,0:T(8,128)(2,1)} %states.1) | copy-start | bytes 1179652

commit v3 on v2

--- a/solution.py
+++ b/solution.py
@@ -70,6 +70,7 @@
     part_in,
     gmine,
     gout,
+    scores,
     s_tab,
     r_tab,
     s_cand,
@@ -237,28 +238,6 @@
             qpad[b * heads + 2 * j] = jnp.where(low, qb, 0.0).astype(jnp.bfloat16)
             qpad[b * heads + 2 * j + 1] = jnp.where(low, swap_halves(qb), 0.0).astype(jnp.bfloat16)
 
-    each_peer(lambda d: tab_copy(d, d).wait_recv())
-    table = pltpu.make_async_copy(tab, tab_s, l_sem)
-    table.start()
-    table.wait()
-
-    def serve(d):
-        for c in range(cap):
-            stage[d * cap + c] = kvb[tab_s[d, 0, c]]
-        rand_copy(d, me).start()
-
-    def serve_some(start, stop):
-        def step(k, carry):
-            serve(peer(k))
-            return carry
-
-        lax.fori_loop(start, stop, step, 0)
-
-    batch = 1 + n // 3
-    serve_some(1, batch)
-    for c in range(cap):
-        rr[me * cap + c] = kvb[tab_s[me, 0, c]]
-
     def relay():
         each_peer(lambda d: cand_copy(d, d, me).wait_recv())
         for u in range(per):
@@ -274,6 +253,28 @@
         each_peer(lambda d: gath_copy(d, me).start())
 
     guarded(cand_parts, me, relay)
+
+    each_peer(lambda d: tab_copy(d, d).wait_recv())
+    table = pltpu.make_async_copy(tab, tab_s, l_sem)
+    table.start()
+    table.wait()
+
+    def serve(d):
+        for c in range(cap):
+            stage[d * cap + c] = kvb[tab_s[d, 0, c]]
+        rand_copy(d, me).start()
+
+    def serve_some(start, stop):
+        def step(k, carry):
+            serve(peer(k))
+            return carry
+
+        lax.fori_loop(start, stop, step, 0)
+
+    batch = n // 2
+    serve_some(1, batch)
+    for c in range(cap):
+        rr[me * cap + c] = kvb[tab_s[me, 0, c]]
 
     each_peer(lambda d: guarded(cand_parts, d, lambda: gath_copy(d, d).wait_recv()))
     for k in range(1, half):
@@ -330,6 +331,24 @@
     win[heads : heads + blocks * heads] = kvb[...]
     win[heads + blocks * heads :] = halo_r[...]
 
+    near = 3 + g_count
+    slot_lane = lax.broadcasted_iota(jnp.int32, (BS, near * BS), 1)
+
+    def near_keys(at, h):
+        return jnp.concatenate([win[at + t * heads] for t in range(3)] + [gkv[h]], axis=0)
+
+    def near_step(b, carry):
+        first = me * blocks + b
+        start = jnp.where(first == 0, BS, 0)
+        stop = jnp.where(first == n * blocks - 1, 2 * BS, 3 * BS)
+        outside = (slot_lane < start) | ((slot_lane >= stop) & (slot_lane < 3 * BS))
+        for h in range(heads):
+            at = b * heads + h
+            scores[at] = jnp.where(outside, NEGATIVE, dot_t(qpad[at], near_keys(at, h)))
+        return carry
+
+    lax.fori_loop(0, blocks, near_step, 0)
+
     def combine():
         part_in[me] = part[me]
         each_peer(lambda d: part_copy(d, d, me).wait_recv())
@@ -363,28 +382,27 @@
 
     each_peer(lambda d: rand_copy(d, d).wait_recv())
 
-    slots = 3 + R + g_count
-    slot_lane = lax.broadcasted_iota(jnp.int32, (BS, slots * BS), 1)
-
     def block_step(b, carry):
-        first = me * blocks + b
-        start = jnp.where(first == 0, BS, 0)
-        stop = jnp.where(first == n * blocks - 1, 2 * BS, 3 * BS)
-        outside = (slot_lane < start) | ((slot_lane >= stop) & (slot_lane < 3 * BS))
         for j in range(pairs):
             halves = []
             for h in (2 * j, 2 * j + 1):
                 at = b * heads + h
-                keys = jnp.concatenate(
-                    [win[at + t * heads] for t in range(3)]
-                    + [rr[slot[at * R + r]] for r in range(R)]
-                    + [gkv[h]],
-                    axis=0,
+                early_keys = near_keys(at, h)
+                keys = jnp.concatenate([rr[slot[at * R + r]] for r in range(R)], axis=0)
+                s = dot_t(qpad[at], keys)
+                early_s = scores[at]
+                high = jnp.maximum(
+                    jnp.max(s, axis=-1, keepdims=True), jnp.max(early_s, axis=-1, keepdims=True)
                 )
-                s = jnp.where(outside, NEGATIVE, dot_t(qpad[at], keys))
-                e = jnp.exp(s - jnp.max(s, axis=-1, keepdims=True))
-                w = (e * (1.0 / jnp.sum(e, axis=-1, keepdims=True))).astype(jnp.bfloat16)
-                halves.append(dot(w, keys))
+                e = jnp.exp(s - high)
+                early_e = jnp.exp(early_s - high)
+                total = jnp.sum(e, axis=-1, keepdims=True) + jnp.sum(
+                    early_e, axis=-1, keepdims=True
+                )
+                share = 1.0 / total
+                w = (e * share).astype(jnp.bfloat16)
+                early_w = (early_e * share).astype(jnp.bfloat16)
+                halves.append(dot(w, keys) + dot(early_w, early_keys))
             att[j, pl.ds(pl.multiple_of(b * BS, BS), BS), :] = jnp.where(
                 low, swap_halves(halves[0]), halves[1]
             ).astype(jnp.bfloat16)
@@ -567,6 +585,7 @@
             pltpu.VMEM((n, 2, rows_per, LANES), bf),
             pltpu.VMEM((rows_per, LANES), bf),
             pltpu.VMEM((parts, rows_per, LANES), bf),
+            pltpu.VMEM((own, BS, (3 + g_count) * BS), jnp.float32),
         ]
         + [dma((n,))] * 8
         + [dma((2,))] * 2

time: 83.4 us -> 84.1 us (level)
  Pallas kernels: 77.1 us -> 78 us
    pallas_call x1, Pallas kernels: 68.7 us -> 70.1 us  [shards(): pl.pallas_call(functools.partial(attend_kernel, n, cap, heads, blocks, g_...]
where the time goes in v3:
time: 84.1 us; the launch traced here: 83.2 us
  Pallas kernels  78 us (93%)
  local copies, waits for them, and re-layouts  3.99 us (5%)
  other arithmetic  1.09 us (1%)
    pallas_call x1, Pallas kernels, shards(): pl.pallas_call(functools.partial(attend_kernel, n, cap, heads, blocks, g_...  70.1 us
    pallas_call x1, Pallas kernels, shards(): pl.pallas_call(functools.partial(tail_kernel, chunks), out_shape=jax.Shap...  7.93 us
    unnamed x12, local copies, waits for them, and re-layouts  2.21 us

profile of v3, /device:TPU:31, one launch (start us, length us, event | category | flops | bytes accessed | tf_op | source)
XLA Modules:
  0.0 83.2 jit_solution(16339687799321452096)
XLA Ops:
  0.0 0.7 reshape.66.gain1
  0.7 0.7 reshape.67.gain2
  1.4 0.7 broadcast_multiply_fusion
  2.1 0.1 iota_add_fusion
  2.1 0.1 copy.16
  2.3 0.1 mul.42
  2.4 0.8 copy.15
  3.2 0.1 reshape.63
  3.3 0.2 convert_reduce_fusion
  3.5 0.1 reshape.64
  3.6 0.1 select_reduce_fusion
  3.7 0.0 copy-start.4
  3.7 0.6 copy-done.4
  4.4 0.0 copy-start
  4.4 0.0 copy-start.1
  4.4 0.0 copy-start.2
  4.4 0.0 copy-start.3
  4.4 70.1 %shard_map.100.att = bf16[3,256,128]{2,1,0:T(8,128)(2,1)S(1)} custom-call(bf16[256,768]{1,0:T(8,128)(2,1)} %states.1, bf16[3,768,384]{2,1,0:T(8,128)(2,1)} %weight_hbm.1, s32[16,1,128]{2,1,0:T(1,128)S(1)} %bitcast.1, s32[72]{0:T(128)S(1)} %get-tuple-element.5.slot, s32[2]{0:T(128)S(1)} %copy-done.4), custom_call_target="tpu_custom_call" | custom-call | flops 30000001024 | bytes 20000000 | tf_op jit(solution)/shard_map/pallas_call | solution.py:558
  74.5 0.0 copy-done
  74.5 0.0 copy-done.1
  74.5 0.0 copy-done.2
  74.5 0.0 copy-done.3
  74.5 7.9 %shard_map.101 = bf16[256,768]{1,0:T(8,128)(2,1)S(1)} custom-call(bf16[3,256,128]{2,1,0:T(8,128)(2,1)S(1)} %shard_map.100.att, bf16[256,768]{1,0:T(8,128)(2,1)S(1)} %copy-done.3, bf16[384,768]{1,0:T(8,128)(2,1)S(1)} %copy-done.2, bf16[768,1536]{1,0:T(8,128)(2,1)S(1)} %copy-done, bf16[1536,768]{1,0:T(8,128)(2,1)S(1)} %copy-done.1, ...), custom_call_target="tpu_custom_call" | custom-call | tf_op jit(solution)/shard_map/pallas_call | solution.py:612
  82.4 0.7 copy.18
  (4 shorter events, 0.0 us)
Async XLA Ops:
  3.7 0.7 copy-start.4
  4.4 70.1 %copy-start = (bf16[768,1536]{1,0:T(8,128)(2,1)S(1)}, bf16[768,1536]{1,0:T(8,128)(2,1)}, u32[]{:S(2)}) copy-start(bf16[768,1536]{1,0:T(8,128)(2,1)} %up_w.1) | copy-start | bytes 7077892
  4.4 70.1 %copy-start.1 = (bf16[1536,768]{1,0:T(8,128)(2,1)S(1)}, bf16[1536,768]{1,0:T(8,128)(2,1)}, u32[]{:S(2)}) copy-start(bf16[1536,768]{1,0:T(8,128)(2,1)} %down_w.1) | copy-start | bytes 7077892
  4.4 70.1 %copy-start.2 = (bf16[384,768]{1,0:T(8,128)(2,1)S(1)}, bf16[384,768]{1,0:T(8,128)(2,1)}, u32[]{:S(2)}) copy-start(bf16[384,768]{1,0:T(8,128)(2,1)} %out_w.1) | copy-start | bytes 1769476
  4.4 70.1 %copy-start.3 = (bf16[256,768]{1,0:T(8,128)(2,1)S(1)}, bf16[256,768]{1,0:T(8,128)(2,1)}, u32[]{:S(2)}) copy-start(bf16[256,768]{1,0:T(8,128)(2,1)} %states.1) | copy-start | bytes 1179652

commit v4 on v3

--- a/solution.py
+++ b/solution.py
@@ -271,8 +271,6 @@
 
         lax.fori_loop(start, stop, step, 0)
 
-    batch = n // 2
-    serve_some(1, batch)
     for c in range(cap):
         rr[me * cap + c] = kvb[tab_s[me, 0, c]]
 
@@ -323,7 +321,7 @@
         for c in range(cuts):
             part[(h // 2) * cuts + c, h % 2] = packed[c * rows_per : (c + 1) * rows_per]
     each_peer(lambda d: guarded(part_parts, d, lambda: part_copy(d, me, d).start()))
-    serve_some(batch, n)
+    serve_some(1, n)
 
     to_right.wait_recv()
     to_left.wait_recv()

time: 84.1 us -> 78.2 us (0.930)
  the two profiles are of different devices: /device:TPU:31 before, /device:TPU:15 now
where the time goes in v4:
time: 78.2 us; the launch traced here: 77.9 us
  Pallas kernels  72.7 us (93%)
  local copies, waits for them, and re-layouts  3.99 us (5%)
  other arithmetic  1.09 us (1%)
    pallas_call x1, Pallas kernels, shards(): pl.pallas_call(functools.partial(attend_kernel, n, cap, heads, blocks, g_...  65.2 us
    pallas_call x1, Pallas kernels, shards(): pl.pallas_call(functools.partial(tail_kernel, chunks), out_shape=jax.Shap...  7.51 us
    unnamed x12, local copies, waits for them, and re-layouts  2.21 us

profile of v4, /device:TPU:15, one launch (start us, length us, event | category | flops | bytes accessed | tf_op | source)
XLA Modules:
  0.0 77.9 jit_solution(16122870020571309998)
XLA Ops:
  0.0 0.7 reshape.66.gain1
  0.7 0.7 reshape.67.gain2
  1.4 0.7 broadcast_multiply_fusion
  2.1 0.1 iota_add_fusion
  2.1 0.1 copy.16
  2.3 0.1 mul.42
  2.4 0.8 %copy.15 = s32[1,4,6,3]{3,2,1,0:T(8,128)S(1)} copy(s32[1,4,6,3]{2,1,3,0:T(4,128)} %param.18) | data formatting | bytes 576 | tf_op args[8]
  3.2 0.1 reshape.63
  3.3 0.2 convert_reduce_fusion
  3.5 0.1 reshape.64
  3.6 0.1 select_reduce_fusion
  3.7 0.0 copy-start.4
  3.7 0.6 copy-done.4
  4.4 0.0 copy-start
  4.4 0.0 copy-start.1
  4.4 0.0 copy-start.2
  4.4 0.0 copy-start.3
  4.4 65.2 %shard_map.100.att = bf16[3,256,128]{2,1,0:T(8,128)(2,1)S(1)} custom-call(bf16[256,768]{1,0:T(8,128)(2,1)} %states.1, bf16[3,768,384]{2,1,0:T(8,128)(2,1)} %weight_hbm.1, s32[16,1,128]{2,1,0:T(1,128)S(1)} %bitcast.1, s32[72]{0:T(128)S(1)} %get-tuple-element.5.slot, s32[2]{0:T(128)S(1)} %copy-done.4), custom_call_target="tpu_custom_call" | custom-call | flops 30000001024 | bytes 20000000 | tf_op jit(solution)/shard_map/pallas_call | solution.py:556
  69.6 0.0 copy-done
  69.6 0.0 copy-done.1
  69.6 0.0 copy-done.2
  69.6 0.0 copy-done.3
  69.6 7.5 %shard_map.101 = bf16[256,768]{1,0:T(8,128)(2,1)S(1)} custom-call(bf16[3,256,128]{2,1,0:T(8,128)(2,1)S(1)} %shard_map.100.att, bf16[256,768]{1,0:T(8,128)(2,1)S(1)} %copy-done.3, bf16[384,768]{1,0:T(8,128)(2,1)S(1)} %copy-done.2, bf16[768,1536]{1,0:T(8,128)(2,1)S(1)} %copy-done, bf16[1536,768]{1,0:T(8,128)(2,1)S(1)} %copy-done.1, ...), custom_call_target="tpu_custom_call" | custom-call | tf_op jit(solution)/shard_map/pallas_call | solution.py:610
  77.1 0.7 copy.18
  (4 shorter events, 0.0 us)
Async XLA Ops:
  3.7 0.7 copy-start.4
  4.4 65.2 %copy-start = (bf16[768,1536]{1,0:T(8,128)(2,1)S(1)}, bf16[768,1536]{1,0:T(8,128)(2,1)}, u32[]{:S(2)}) copy-start(bf16[768,1536]{1,0:T(8,128)(2,1)} %up_w.1) | copy-start | bytes 7077892
  4.4 65.2 %copy-start.1 = (bf16[1536,768]{1,0:T(8,128)(2,1)S(1)}, bf16[1536,768]{1,0:T(8,128)(2,1)}, u32[]{:S(2)}) copy-start(bf16[1536,768]{1,0:T(8,128)(2,1)} %down_w.1) | copy-start | bytes 7077892
  4.4 65.2 %copy-start.2 = (bf16[384,768]{1,0:T(8,128)(2,1)S(1)}, bf16[384,768]{1,0:T(8,128)(2,1)}, u32[]{:S(2)}) copy-start(bf16[384,768]{1,0:T(8,128)(2,1)} %out_w.1) | copy-start | bytes 1769476
  4.4 65.2 %copy-start.3 = (bf16[256,768]{1,0:T(8,128)(2,1)S(1)}, bf16[256,768]{1,0:T(8,128)(2,1)}, u32[]{:S(2)}) copy-start(bf16[256,768]{1,0:T(8,128)(2,1)} %states.1) | copy-start | bytes 1179652
